TPU v7x, 32 devices: a whole 2x2x4 slice. The times are simulated.
32 devices in a mesh: row: 4 (over z), col: 8 (over y, x, core).
Axes of the slice: x: 2, y: 2, z: 4, core: 2. Of those that a mesh axis runs over, the one named last changes fastest.
Arguments:
- front: float32 [12288, 12288], P('row', 'col'), as said below
- structure: int32 [3, 96], replicated, may hold values from 0 to 1, as said below
- factor_front: float32 [3, 12288, 512], P(None, 'row', 'col'), may hold values from -0.0546875 to 0.0546875
- factor_border: float32 [2, 512, 512], replicated, may hold values from -0.6 to 0.6
- pivot_inverse: float32 [3, 512, 512], P(None, 'row')
Outputs:
- inverse_front: float32 [3, 512, 12288], P(None, 'row', 'col')
- inverse_parent: float32 [2, 512, 512], P(None, 'row')
- inverse_diagonal: float32 [3, 512, 512], P(None, 'row')
Inputs may be any that keep to these rules, and one draw needn't show every extreme that they name: front is exactly symmetric. structure[k, b] = 1 where front block b (rows b * 128 to (b + 1) * 128 - 1) lies in supernode k's structure; every 1 in row k is also a 1 in row k - 1; blocks b < 24 are 1 in every row.
All inputs are finite; a program needn't handle non-finite values.
Results may differ from a plain program's by a relative error of at most 0.0001.
Values sent between devices are 32-bit elements; how exact they have to be, the bound alone decides.
No kernel may reach another device: no remote copies, remote signals or barrier semaphores. Data moves between devices by JAX's collectives and lax.ppermute only.
A program may use at most 128 MiB of HBM per device.

v0:
```python
import jax
import jax.numpy as jnp
from jax import lax
from jax.sharding import PartitionSpec as P

BLK = 128
HIGH = lax.Precision.HIGHEST


def broadcast(x, axis, root):
    mine = lax.axis_index(axis) == root
    return lax.psum(jnp.where(mine, x, jnp.zeros_like(x)), axis)


def matmul(former, latter):
    return jnp.dot(former, latter, precision=HIGH, preferred_element_type=jnp.float32)


def contract_first(former, latter):
    return lax.dot_general(
        former, latter, (((0,), (0,)), ((), ())), precision=HIGH, preferred_element_type=jnp.float32
    )


def block_flags(structure_row, first_row, rows_count):
    position = first_row + jnp.arange(rows_count, dtype=jnp.int32)
    owners = position // BLK
    numbers = jnp.arange(structure_row.shape[0], dtype=jnp.int32)
    matches = (owners[:, None] == numbers[None, :]).astype(jnp.float32)
    return jnp.dot(matches, structure_row.astype(jnp.float32), precision=HIGH)


def body(front, structure, factor_front, factor_border, pivot_inverse):
    row_index = lax.axis_index("row")
    col_index = lax.axis_index("col")
    rows_here = front.shape[0]
    cols_here = front.shape[1]
    width_here = pivot_inverse.shape[1]
    supers = structure.shape[0]
    row_first = row_index * rows_here
    col_first = col_index * cols_here
    fronts = []
    parents = []
    diagonals = []
    previous = None
    diag_prev = None
    for section in range(supers):
        gathered = lax.all_gather(factor_front[section], "col", axis=1, tiled=True)
        row_flags = block_flags(structure[section], row_first, rows_here)
        factor_rows = gathered * row_flags[:, None]
        own_half = lax.dynamic_slice_in_dim(factor_rows, col_index % 2 * cols_here, cols_here, 0)
        factor_cols = broadcast(own_half, "row", col_index // 2)
        partial_value = contract_first(factor_rows, front)
        if section > 0:
            border = factor_border[section - 1]
            border_rows = lax.dynamic_slice_in_dim(border, row_index * width_here, width_here, 0)
            partial_value = partial_value + contract_first(border_rows, previous)
            parent_part = lax.psum(matmul(previous, factor_cols), "col")
            parent_rows = parent_part + matmul(diag_prev, border)
            parent_all = lax.all_gather(parent_rows, "row", axis=0, tiled=True)
            parents.append(-parent_rows)
        image_rows = lax.psum_scatter(partial_value, "row", scatter_dimension=0, tiled=True)
        col_flags = block_flags(structure[section], col_first, cols_here)
        current = -(image_rows * col_flags[None, :])
        gram_rows = lax.psum(matmul(image_rows, factor_cols), "col")
        diag_now = pivot_inverse[section] + gram_rows
        if section > 0:
            parent_slice = lax.dynamic_slice_in_dim(
                parent_all, row_index * width_here, width_here, 1
            )
            diag_now = diag_now + contract_first(parent_slice, border)
        fronts.append(current)
        diagonals.append(diag_now)
        previous = current
        diag_prev = diag_now
    return (jnp.stack(fronts), jnp.stack(parents), jnp.stack(diagonals))


def solution(mesh):
    placed = (P("row", "col"), P(), P(None, "row", "col"), P(), P(None, "row", None))
    return jax.shard_map(
        body,
        mesh=mesh,
        in_specs=placed,
        out_specs=(P(None, "row", "col"), P(None, "row", None), P(None, "row", None)),
        check_vma=False,
    )
```

profile of v0, /device:TPU:0, one launch (start us, length us, event | category | flops | bytes accessed | tf_op | source)
XLA Modules:
  0.0 802.7 jit_solution(8092300581253794925)
XLA Ops:
  7.2 3.1 fusion.61
  10.4 0.7 all-gather.15.cloned.1.call-update
  11.2 2.0 fusion.2
  13.2 45.4 %all-gather.13.cloned.1.call-done = f32[1,3072,512]{1,2,0:T(8,128)} async-done(((f32[1,3072,64]{1,2,0:T(8,128)}), f32[1,3072,512]{1,2,0:T(8,128)}) %all-gather.13.cloned.1.call-update) | async-done | bytes 6291472 | tf_op jit(solution)/shard_map/all_gather | solution.py:48
  58.6 3.4 bitcast_multiply_fusion.2
  62.0 2.6 copy-done.1
  64.7 33.4 %fusion.63 = f32[512,1536]{1,0:T(8,128)} fusion(f32[3072,512]{0,1:T(8,128)S(1)} %bitcast_multiply_fusion.2, f32[3072,1536]{1,0:T(8,128)} %param.5), kind=kOutput, calls=%fused_computation.103 | convolution fusion | flops 28991029248 | bytes 28311552 | tf_op jit(solution)/shard_map/dot_general | solution.py:20
  99.2 0.6 convolution_reduce_fusion.2
  99.9 2.0 fusion.1
  101.9 1.1 fusion.62
  103.0 2.9 all-gather.15.cloned.1.call-done
  105.9 3.4 bitcast_multiply_fusion.1
  109.3 2.6 copy-done.2
  111.9 33.4 %fusion.64 = f32[512,1536]{1,0:T(8,128)} fusion(f32[3072,512]{0,1:T(8,128)S(1)} %bitcast_multiply_fusion.1, f32[3072,1536]{1,0:T(8,128)} %param.5), kind=kOutput, calls=%fused_computation.104 | convolution fusion | flops 28991029248 | bytes 28311552 | tf_op jit(solution)/shard_map/dot_general | solution.py:20
  145.3 23.4 %reduce-scatter.4.cloned.1.call-done = f32[128,1536]{1,0:T(8,128)} async-done(((f32[512,1536]{1,0:T(8,128)}), f32[128,1536]{1,0:T(8,128)}) %reduce-scatter.4.cloned.1.call-update) | async-done | bytes 786448 | tf_op jit(solution)/shard_map/reduce_scatter | solution.py:62
  168.6 6.6 convolution_add_fusion.1
  175.5 2.0 fusion
  177.5 4.1 dynamic-slice_select_fusion.2
  181.6 3.8 dynamic-slice_select_fusion.1
  185.4 30.3 %all-gather.17.cloned.1.call-done = f32[1,3072,512]{1,2,0:T(8,128)} async-done(((f32[1,3072,64]{1,2,0:T(8,128)}), f32[1,3072,512]{1,2,0:T(8,128)}) %all-gather.17.cloned.1.call-update) | async-done | bytes 6291472 | tf_op jit(solution)/shard_map/all_gather | solution.py:48
  215.7 3.4 bitcast_multiply_fusion
  219.1 2.6 copy-done.3
  221.8 1.9 dynamic-slice_select_fusion
  223.8 0.6 convolution_reduce_fusion.1
  224.4 35.4 %fusion.65 = f32[512,1536]{1,0:T(8,128)} fusion(f32[3072,512]{0,1:T(8,128)} %copy-done.3, f32[3072,1536]{1,0:T(8,128)} %param.5), kind=kOutput, calls=%fused_computation.105 | convolution fusion | flops 28991029248 | bytes 28311552 | tf_op jit(solution)/shard_map/dot_general | solution.py:20
  259.8 18.5 %reduce-scatter.6.cloned.1.call-done = f32[128,1536]{1,0:T(8,128)} async-done(((f32[512,1536]{1,0:T(8,128)}), f32[128,1536]{1,0:T(8,128)}) %reduce-scatter.6.cloned.1.call-update) | async-done | bytes 786448 | tf_op jit(solution)/shard_map/reduce_scatter | solution.py:62
  278.3 5.6 convolution_add_fusion
  284.2 321.4 %all-reduce.7.cloned.1.call-done = (f32[1536,512]{0,1:T(8,128)}, f32[1536,512]{0,1:T(8,128)}, f32[1536,512]{0,1:T(8,128)}) async-done(((f32[1536,512]{0,1:T(8,128)}, f32[1536,512]{0,1:T(8,128)}, f32[1536,512]{0,1:T(8,128)}), (f32[1536,512]{0,1:T(8,128)}, f32[1536,512]{0,1:T(8,128)}, f32[1536,512]{0,1:T(8,128)})) %all-reduce.7.cloned.1.call-update) | async-done | bytes 9437200 | tf_op jit(solution)/shard_map/psum | solution.py:12
  605.6 6.0 fusion.66
  611.6 3.9 fusion.11
  615.5 4.0 fusion.67
  619.6 3.9 fusion.13
  623.4 43.9 %reduce-scatter.8.cloned.1.call-done = f32[128,1536]{1,0:T(8,128)} async-done(((f32[512,1536]{1,0:T(8,128)}), f32[128,1536]{1,0:T(8,128)}) %reduce-scatter.8.cloned.1.call-update) | async-done | bytes 786448 | tf_op jit(solution)/shard_map/reduce_scatter | solution.py:62
  667.3 6.1 fusion.68
  673.8 58.5 %all-reduce.5.cloned.1.call-done = (f32[128,512]{1,0:T(8,128)}, f32[128,512]{1,0:T(8,128)}, f32[128,512]{1,0:T(8,128)}, f32[128,512]{1,0:T(8,128)}, f32[128,512]{1,0:T(8,128)}) async-done(((f32[128,512]{1,0:T(8,128)}, f32[128,512]{1,0:T(8,128)}, f32[128,512]{1,0:T(8,128)}, f32[128,512]{1,0:T(8,128)}, f32[128,512]{1,0:T(8,128)}), (f32[128,512]{1,0:T(8,128)}, f32[128,512]{1,0:T(8,128)}, f32[128,512]{1,0:T(8,128)}, ...) | async-done | bytes 1310736 | tf_op jit(solution)/shard_map/psum | solution.py:58
  732.3 2.5 convolution_add_fusion.5
  734.9 0.6 convolution_reduce_fusion
  735.5 1.0 fusion.12
  736.5 2.2 fusion.14
  738.7 23.4 %all-gather.9.cloned.1.call-done = f32[512,512]{1,0:T(8,128)} async-done(((f32[128,512]{1,0:T(8,128)}), f32[512,512]{1,0:T(8,128)}) %all-gather.9.cloned.1.call-update) | async-done | bytes 1048592 | tf_op jit(solution)/shard_map/all_gather | solution.py:60
  762.1 1.9 convolution_add_fusion.4
  764.0 1.4 convolution_add_fusion.3
  765.5 3.0 pad_maximum_fusion
  768.6 1.0 fusion.28
  769.6 0.8 pad_maximum_fusion.2
  770.4 22.5 %all-gather.11.cloned.1.call-done = f32[512,512]{1,0:T(8,128)} async-done(((f32[128,512]{1,0:T(8,128)}), f32[512,512]{1,0:T(8,128)}) %all-gather.11.cloned.1.call-update) | async-done | bytes 1048592 | tf_op jit(solution)/shard_map/all_gather | solution.py:60
  792.9 1.8 fusion.3
  794.7 0.9 pad_maximum_fusion.1
  (51 shorter events, 2.4 us)
Async XLA Ops:
  7.2 4.0 copy-start.14
  7.2 51.4 %all-gather.13.cloned.1.call-start = ((), (), s32[]{:S(2)}) async-start(), calls=%async_computation.8 | async-start | bytes 7077888 | tf_op jit(solution)/shard_map/all_gather | solution.py:48
  10.3 95.6 %all-gather.15.cloned.1.call-start = ((), (), s32[]{:S(2)}) async-start(), calls=%async_computation.9 | async-start | bytes 7077888 | tf_op jit(solution)/shard_map/all_gather | solution.py:48
  11.1 157.6 %reduce-scatter.4.cloned.1.call-start = ((), (), s32[]{:S(2)}) async-start(), calls=%async_computation.3 | async-start | bytes 3932160 | tf_op jit(solution)/shard_map/reduce_scatter | solution.py:62
  62.0 2.7 copy-start.1
  98.0 3.8 copy-start
  98.1 117.6 %all-gather.17.cloned.1.call-start = ((), (), s32[]{:S(2)}) async-start(), calls=%async_computation.10 | async-start | bytes 7077888 | tf_op jit(solution)/shard_map/all_gather | solution.py:48
  98.6 179.6 %reduce-scatter.6.cloned.1.call-start = ((), (), s32[]{:S(2)}) async-start(), calls=%async_computation.4 | async-start | bytes 3932160 | tf_op jit(solution)/shard_map/reduce_scatter | solution.py:62
  109.3 2.6 copy-start.2
  175.3 430.3 %all-reduce.7.cloned.1.call-start = ((), (), s32[]{:S(2)}) async-start(), calls=%async_computation.12 | async-start | bytes 18874368 | tf_op jit(solution)/shard_map/psum | solution.py:12
  219.1 2.7 copy-start.3
  223.7 443.5 %reduce-scatter.8.cloned.1.call-start = ((), (), s32[]{:S(2)}) async-start(), calls=%async_computation.5 | async-start | bytes 3932160 | tf_op jit(solution)/shard_map/reduce_scatter | solution.py:62
  283.9 321.7 %copy-start.4 = (f32[128,1536]{1,0:T(8,128)S(1)}, f32[128,1536]{1,0:T(8,128)}, u32[]{:S(2)}) copy-start(f32[128,1536]{1,0:T(8,128)} %reduce-scatter.4.cloned.1.call-done) | copy-start | bytes 2359300
  284.0 448.3 %all-reduce.5.cloned.1.call-start = ((), (), s32[]{:S(2)}) async-start(), calls=%async_computation.11 | async-start | bytes 2621440 | tf_op jit(solution)/shard_map/psum | solution.py:58
  605.6 6.0 copy-start.7
  611.6 3.9 copy-start.5
  615.5 4.0 copy-start.6
  673.5 88.6 %all-gather.9.cloned.1.call-start = ((), (), s32[]{:S(2)}) async-start(), calls=%async_computation.6 | async-start | bytes 1310720 | tf_op jit(solution)/shard_map/all_gather | solution.py:60
  734.8 29.1 %copy-start.13 = (f32[128,512]{1,0:T(8,128)S(1)}, f32[128,512]{1,0:T(8,128)}, u32[]{:S(2)}) copy-start(f32[128,512]{1,0:T(8,128)} %get-tuple-element.3) | copy-start | bytes 786436
  734.8 58.1 %all-gather.11.cloned.1.call-start = ((), (), s32[]{:S(2)}) async-start(), calls=%async_computation.7 | async-start | bytes 1310720 | tf_op jit(solution)/shard_map/all_gather | solution.py:60
  736.5 28.9 %copy-start.8 = (f32[128,1536]{1,0:T(8,128)S(1)}, f32[128,1536]{1,0:T(8,128)}, u32[]{:S(2)}) copy-start(f32[128,1536]{1,0:T(8,128)} %reduce-scatter.8.cloned.1.call-done) | copy-start | bytes 2359300
  765.4 3.1 copy-start.10
  765.4 3.1 copy-start.11
  765.5 4.0 copy-start.9
  765.5 27.4 %copy-start.12 = (f32[128,512]{1,0:T(8,128)S(1)}, f32[128,512]{1,0:T(8,128)}, u32[]{:S(2)}) copy-start(f32[128,512]{1,0:T(8,128)} %get-tuple-element.7) | copy-start | bytes 786436
Sparse Core Ops, SparseCore 0:
  10.5 48.1 all-gather.12
  60.5 45.3 all-gather.14
  108.2 60.3 reduce-scatter.3
  170.4 45.2 all-gather.16
  217.9 60.3 reduce-scatter.5
  281.0 324.5 all-reduce.6
  607.9 59.3 reduce-scatter.7
  673.6 58.6 all-reduce.4
  735.0 27.0 all-gather.8
  765.5 27.3 all-gather.10
where the time goes:
time: 809 us; the launch traced here: 803 us
  waiting for transfers between devices  591 us (73%)
  matrix products  154 us (19%)
  other arithmetic  29 us (4%)
  between operations  14.7 us (2%)
  local copies, waits for them, and re-layouts  12.1 us (1%)
    psum x1, waiting for transfers between devices, broadcast(): return lax.psum(jnp.where(mine, x, jnp.zeros_like(x)), axis)  321 us
    dot_general x7, matrix products, contract_first(): lax.dot_general(former, latter, (((0,), (0,)), ((), ())), precision=HIGH,...  118 us
    reduce_scatter x3, waiting for transfers between devices, body(): lax.psum_scatter(partial_value, 'row', scatter_dimension=0, tiled=True)  85.7 us
    all_gather x3, waiting for transfers between devices, body(): gathered = lax.all_gather(factor_front[section], 'col', axis=1, tiled=True)  78.7 us
    psum x1, waiting for transfers between devices, body(): parent_part = lax.psum(matmul(previous, factor_cols), 'col')  58.5 us
    all_gather x2, waiting for transfers between devices, body(): parent_all = lax.all_gather(parent_rows, 'row', axis=0, tiled=True)  45.9 us
    dot_general x7, matrix products, matmul(): jnp.dot(former, latter, precision=HIGH, preferred_element_type=jnp.float32)  27.9 us
  transfers between devices with their start and end apart: 10, of which 10 were waited for; matrix products, arithmetic and copies ran while one was open for 21% of the time, Pallas kernels for 0%

commit v1 on v0

--- a/solution.py
+++ b/solution.py
@@ -9,7 +9,7 @@
 
 def broadcast(x, axis, root):
     mine = lax.axis_index(axis) == root
-    return lax.psum(jnp.where(mine, x, jnp.zeros_like(x)), axis)
+    return jnp.sum(lax.all_gather(jnp.where(mine, x, jnp.zeros_like(x)), axis), axis=0)
 
 
 def matmul(former, latter):

time: 809 us -> 1140 us (1.41)
  waiting for transfers between devices: 591 us -> 841 us
  local copies, waits for them, and re-layouts: 12.1 us -> 60.2 us
  other arithmetic: 29 us -> 65.4 us
    all_gather x0 -> x3, waiting for transfers between devices: none -> 594 us  [broadcast(): lax.all_gather(jnp.where(mine, x, jnp.zeros_like(x)), axis)]
    psum x1 -> x0, waiting for transfers between devices: 321 us -> none  [broadcast(): return lax.psum(jnp.where(mine, x, jnp.zeros_like(x)), axis)]
    all_gather x0 -> x3, local copies, waits for them, and re-layouts: none -> 47.7 us  [broadcast(): lax.all_gather(jnp.where(mine, x, jnp.zeros_like(x)), axis)]
    reduce_sum x0 -> x3, other arithmetic: none -> 36.5 us  [broadcast(): jnp.sum(lax.all_gather(jnp.where(mine, x, jnp.zeros_like(x)), axis), axis=0)]
    reduce_scatter x3, waiting for transfers between devices: 85.7 us -> 53.3 us  [body(): lax.psum_scatter(partial_value, 'row', scatter_dimension=0, tiled=True)]
  transfers between devices with their start and end apart: 10 -> 12, of which waited for: 10 -> 12; matrix products, arithmetic and copies ran while one was open for 21% -> 22% of each run, Pallas kernels for 0% -> 0%
where the time goes in v1:
time: 1140 us; the launch traced here: 1130 us
  waiting for transfers between devices  841 us (74%)
  matrix products  151 us (13%)
  other arithmetic  65.4 us (6%)
  local copies, waits for them, and re-layouts  60.2 us (5%)
  between operations  14.8 us (1%)
    all_gather x3, waiting for transfers between devices, broadcast(): lax.all_gather(jnp.where(mine, x, jnp.zeros_like(x)), axis)  594 us
    dot_general x7, matrix products, contract_first(): lax.dot_general(former, latter, (((0,), (0,)), ((), ())), precision=HIGH,...  116 us
    all_gather x3, waiting for transfers between devices, body(): gathered = lax.all_gather(factor_front[section], 'col', axis=1, tiled=True)  87.6 us
    psum x1, waiting for transfers between devices, body(): parent_part = lax.psum(matmul(previous, factor_cols), 'col')  58.6 us
    reduce_scatter x3, waiting for transfers between devices, body(): lax.psum_scatter(partial_value, 'row', scatter_dimension=0, tiled=True)  53.3 us
    all_gather x3, local copies, waits for them, and re-layouts, broadcast(): lax.all_gather(jnp.where(mine, x, jnp.zeros_like(x)), axis)  47.7 us
    all_gather x2, waiting for transfers between devices, body(): parent_all = lax.all_gather(parent_rows, 'row', axis=0, tiled=True)  45.9 us
    reduce_sum x3, other arithmetic, broadcast(): jnp.sum(lax.all_gather(jnp.where(mine, x, jnp.zeros_like(x)), axis), axis=0)  36.5 us
  transfers between devices with their start and end apart: 12, of which 12 were waited for; matrix products, arithmetic and copies ran while one was open for 22% of the time, Pallas kernels for 0%

profile of v1, /device:TPU:0, one launch (start us, length us, event | category | flops | bytes accessed | tf_op | source)
XLA Modules:
  0.0 1133.4 jit_solution(8649520426344873336)
XLA Ops:
  7.2 3.1 fusion.61
  11.2 2.0 fusion.2
  13.2 45.4 %all-gather.19.cloned.1.call-done = f32[1,3072,512]{1,2,0:T(8,128)} async-done(((f32[1,3072,64]{1,2,0:T(8,128)}), f32[1,3072,512]{1,2,0:T(8,128)}) %all-gather.19.cloned.1.call-update) | async-done | bytes 6291472 | tf_op jit(solution)/shard_map/all_gather | solution.py:48
  58.6 3.4 bitcast_multiply_fusion.2
  62.0 2.6 copy-done.3
  64.7 33.4 %fusion.63 = f32[512,1536]{1,0:T(8,128)} fusion(f32[3072,512]{0,1:T(8,128)S(1)} %bitcast_multiply_fusion.2, f32[3072,1536]{1,0:T(8,128)} %param.5), kind=kOutput, calls=%fused_computation.103 | convolution fusion | flops 28991029248 | bytes 28311552 | tf_op jit(solution)/shard_map/dot_general | solution.py:20
  99.5 2.0 fusion.1
  101.6 1.5 fusion.62
  103.1 2.9 all-gather.21.cloned.1.call-done
  105.9 3.4 bitcast_multiply_fusion.1
  109.3 2.6 copy-done.4
  111.9 34.1 %fusion.64 = f32[512,1536]{1,0:T(8,128)S(1)} fusion(f32[3072,512]{0,1:T(8,128)S(1)} %bitcast_multiply_fusion.1, f32[3072,1536]{1,0:T(8,128)} %param.5), kind=kOutput, calls=%fused_computation.104 | convolution fusion | flops 28991029248 | bytes 28311552 | tf_op jit(solution)/shard_map/dot_general | solution.py:20
  146.0 22.7 %reduce-scatter.4.cloned.1.call-done = f32[128,1536]{1,0:T(8,128)} async-done(((f32[512,1536]{1,0:T(8,128)}), f32[128,1536]{1,0:T(8,128)}) %reduce-scatter.4.cloned.1.call-update) | async-done | bytes 786448 | tf_op jit(solution)/shard_map/reduce_scatter | solution.py:62
  168.7 5.6 convolution_add_fusion.1
  174.4 2.0 fusion
  176.4 39.3 %all-gather.23.cloned.1.call-done = f32[1,3072,512]{1,2,0:T(8,128)} async-done(((f32[1,3072,64]{1,2,0:T(8,128)}), f32[1,3072,512]{1,2,0:T(8,128)}) %all-gather.23.cloned.1.call-update) | async-done | bytes 6291472 | tf_op jit(solution)/shard_map/all_gather | solution.py:48
  215.7 3.4 bitcast_multiply_fusion
  219.1 2.6 copy-done.5
  221.8 1.9 dynamic-slice_select_fusion
  223.7 4.0 dynamic-slice_select_fusion.2
  227.8 3.8 dynamic-slice_select_fusion.1
  232.3 33.8 %fusion.65 = f32[512,1536]{1,0:T(8,128)S(1)} fusion(f32[3072,512]{0,1:T(8,128)} %copy-done.5, f32[3072,1536]{1,0:T(8,128)} %param.5), kind=kOutput, calls=%fused_computation.105 | convolution fusion | flops 28991029248 | bytes 28311552 | tf_op jit(solution)/shard_map/dot_general | solution.py:20
  266.1 12.2 %reduce-scatter.6.cloned.1.call-done = f32[128,1536]{1,0:T(8,128)} async-done(((f32[512,1536]{1,0:T(8,128)}), f32[128,1536]{1,0:T(8,128)}) %reduce-scatter.6.cloned.1.call-update) | async-done | bytes 786448 | tf_op jit(solution)/shard_map/reduce_scatter | solution.py:62
  278.3 5.5 convolution_add_fusion
  283.9 214.0 %all-gather.29.cloned.1.call-done = f32[6144,512]{0,1:T(8,128)} async-done(((f32[1536,512]{0,1:T(8,128)}), f32[6144,512]{0,1:T(8,128)}) %all-gather.29.cloned.1.call-update) | async-done | bytes 12582928 | tf_op jit(solution)/shard_map/all_gather | solution.py:12
  497.9 16.3 %reshape.60 = f32[4,1536,512]{1,0,2:T(4,128)} reshape(f32[6144,512]{0,1:T(8,128)} %all-gather.29.cloned.1.call-done) | data formatting | bytes 25165824 | tf_op jit(solution)/shard_map/all_gather | solution.py:12
  514.1 11.0 reduce_sum.29
  525.1 190.7 %all-gather.25.cloned.1.call-done = f32[6144,512]{0,1:T(8,128)} async-done(((f32[1536,512]{0,1:T(8,128)}), f32[6144,512]{0,1:T(8,128)}) %all-gather.25.cloned.1.call-update) | async-done | bytes 12582928 | tf_op jit(solution)/shard_map/all_gather | solution.py:12
  715.8 15.8 %reshape.58 = f32[4,1536,512]{1,0,2:T(4,128)} reshape(f32[6144,512]{0,1:T(8,128)} %all-gather.25.cloned.1.call-done) | data formatting | bytes 25165824 | tf_op jit(solution)/shard_map/all_gather | solution.py:12
  731.6 12.7 %reduce_sum.27 = f32[1536,512]{0,1:T(8,128)} reduce(f32[4,1536,512]{1,0,2:T(4,128)} %reshape.58, f32[]{:T(128)} %constant.82.clone.1), dimensions={0}, to_apply=%region_3.4 | reduce | flops 2359296 | bytes 15728644 | tf_op jit(solution)/shard_map/reduce_sum | solution.py:12
  744.3 189.5 %all-gather.27.cloned.1.call-done = f32[6144,512]{0,1:T(8,128)} async-done(((f32[1536,512]{0,1:T(8,128)}), f32[6144,512]{0,1:T(8,128)}) %all-gather.27.cloned.1.call-update) | async-done | bytes 12582928 | tf_op jit(solution)/shard_map/all_gather | solution.py:12
  933.8 15.6 %reshape.59 = f32[4,1536,512]{1,0,2:T(4,128)} reshape(f32[6144,512]{0,1:T(8,128)} %all-gather.27.cloned.1.call-done) | data formatting | bytes 25165824 | tf_op jit(solution)/shard_map/all_gather | solution.py:12
  949.4 12.8 %reduce_sum.28 = f32[1536,512]{0,1:T(8,128)} reduce(f32[4,1536,512]{1,0,2:T(4,128)} %reshape.59, f32[]{:T(128)} %constant.82.clone.1), dimensions={0}, to_apply=%region_5.6 | reduce | flops 2359296 | bytes 15728644 | tf_op jit(solution)/shard_map/reduce_sum | solution.py:12
  962.3 6.3 fusion.67
  968.5 3.9 fusion.11
  972.4 3.9 fusion.13
  976.3 18.4 %reduce-scatter.8.cloned.1.call-done = f32[128,1536]{1,0:T(8,128)} async-done(((f32[512,1536]{1,0:T(8,128)}), f32[128,1536]{1,0:T(8,128)}) %reduce-scatter.8.cloned.1.call-update) | async-done | bytes 786448 | tf_op jit(solution)/shard_map/reduce_scatter | solution.py:62
  994.7 5.3 fusion.68
  1000.0 4.0 fusion.66
  1004.4 58.6 %all-reduce.3.cloned.1.call-done = (f32[128,512]{1,0:T(8,128)}, f32[128,512]{1,0:T(8,128)}, f32[128,512]{1,0:T(8,128)}, f32[128,512]{1,0:T(8,128)}, f32[128,512]{1,0:T(8,128)}) async-done(((f32[128,512]{1,0:T(8,128)}, f32[128,512]{1,0:T(8,128)}, f32[128,512]{1,0:T(8,128)}, f32[128,512]{1,0:T(8,128)}, f32[128,512]{1,0:T(8,128)}), (f32[128,512]{1,0:T(8,128)}, f32[128,512]{1,0:T(8,128)}, f32[128,512]{1,0:T(8,128)}, ...) | async-done | bytes 1310736 | tf_op jit(solution)/shard_map/psum | solution.py:58
  1063.0 2.5 convolution_add_fusion.5
  1067.2 2.2 fusion.14
  1069.3 23.4 %all-gather.15.cloned.1.call-done = f32[512,512]{1,0:T(8,128)} async-done(((f32[128,512]{1,0:T(8,128)}), f32[512,512]{1,0:T(8,128)}) %all-gather.15.cloned.1.call-update) | async-done | bytes 1048592 | tf_op jit(solution)/shard_map/all_gather | solution.py:60
  1092.8 1.9 convolution_add_fusion.4
  1094.6 1.4 convolution_add_fusion.3
  1096.2 3.0 pad_maximum_fusion
  1101.1 22.5 %all-gather.17.cloned.1.call-done = f32[512,512]{1,0:T(8,128)} async-done(((f32[128,512]{1,0:T(8,128)}), f32[512,512]{1,0:T(8,128)}) %all-gather.17.cloned.1.call-update) | async-done | bytes 1048592 | tf_op jit(solution)/shard_map/all_gather | solution.py:60
  1123.6 1.8 fusion.3
  (69 shorter events, 8.0 us)
Async XLA Ops:
  7.2 4.0 copy-start.17
  7.2 51.4 %all-gather.19.cloned.1.call-start = ((), (), s32[]{:S(2)}) async-start(), calls=%async_computation.8 | async-start | bytes 7077888 | tf_op jit(solution)/shard_map/all_gather | solution.py:48
  10.4 95.6 %all-gather.21.cloned.1.call-start = ((), (), s32[]{:S(2)}) async-start(), calls=%async_computation.9 | async-start | bytes 7077888 | tf_op jit(solution)/shard_map/all_gather | solution.py:48
  11.1 157.6 %reduce-scatter.4.cloned.1.call-start = ((), (), s32[]{:S(2)}) async-start(), calls=%async_computation.3 | async-start | bytes 3932160 | tf_op jit(solution)/shard_map/reduce_scatter | solution.py:62
  62.0 2.6 copy-start.3
  98.1 3.5 copy-start.1
  98.1 117.6 %all-gather.23.cloned.1.call-start = ((), (), s32[]{:S(2)}) async-start(), calls=%async_computation.10 | async-start | bytes 7077888 | tf_op jit(solution)/shard_map/all_gather | solution.py:48
  98.7 179.6 %reduce-scatter.6.cloned.1.call-start = ((), (), s32[]{:S(2)}) async-start(), calls=%async_computation.4 | async-start | bytes 3932160 | tf_op jit(solution)/shard_map/reduce_scatter | solution.py:62
  109.3 2.6 copy-start.4
  174.3 323.5 %all-gather.29.cloned.1.call-start = ((), (), s32[]{:S(2)}) async-start(), calls=%async_computation.13 | async-start | bytes 15728640 | tf_op jit(solution)/shard_map/all_gather | solution.py:12
  219.1 2.6 copy-start.5
  223.7 492.2 %all-gather.25.cloned.1.call-start = ((), (), s32[]{:S(2)}) async-start(), calls=%async_computation.11 | async-start | bytes 15728640 | tf_op jit(solution)/shard_map/all_gather | solution.py:12
  227.7 706.1 %all-gather.27.cloned.1.call-start = ((), (), s32[]{:S(2)}) async-start(), calls=%async_computation.12 | async-start | bytes 15728640 | tf_op jit(solution)/shard_map/all_gather | solution.py:12
  231.6 763.1 %reduce-scatter.8.cloned.1.call-start = ((), (), s32[]{:S(2)}) async-start(), calls=%async_computation.5 | async-start | bytes 3932160 | tf_op jit(solution)/shard_map/reduce_scatter | solution.py:62
  283.8 779.1 %all-reduce.3.cloned.1.call-start = ((), (), s32[]{:S(2)}) async-start(), calls=%async_computation.14 | async-start | bytes 2621440 | tf_op jit(solution)/shard_map/psum | solution.py:58
  962.3 6.3 copy-start
  962.3 6.3 copy-start.6
  968.5 3.9 copy-start.9
  994.7 5.3 copy-start.7
  994.7 5.3 copy-start.10
  1000.0 62.9 %copy-start.2 = (f32[2,512,512]{2,1,0:T(8,128)S(1)}, f32[2,512,512]{2,1,0:T(8,128)}, u32[]{:S(2)}) copy-start(f32[2,512,512]{2,1,0:T(8,128)} %param.8) | copy-start | bytes 6291460
  1000.0 66.1 %copy-start.8 = (f32[128,1536]{1,0:T(8,128)S(1)}, f32[128,1536]{1,0:T(8,128)}, u32[]{:S(2)}) copy-start(f32[128,1536]{1,0:T(8,128)} %reduce-scatter.4.cloned.1.call-done) | copy-start | bytes 2359300
  1004.1 88.6 %all-gather.15.cloned.1.call-start = ((), (), s32[]{:S(2)}) async-start(), calls=%async_computation.6 | async-start | bytes 1310720 | tf_op jit(solution)/shard_map/all_gather | solution.py:60
  1065.5 29.1 %copy-start.16 = (f32[128,512]{1,0:T(8,128)S(1)}, f32[128,512]{1,0:T(8,128)}, u32[]{:S(2)}) copy-start(f32[128,512]{1,0:T(8,128)} %get-tuple-element.3) | copy-start | bytes 786436
  1065.5 58.1 %all-gather.17.cloned.1.call-start = ((), (), s32[]{:S(2)}) async-start(), calls=%async_computation.7 | async-start | bytes 1310720 | tf_op jit(solution)/shard_map/all_gather | solution.py:60
  1067.2 28.9 %copy-start.11 = (f32[128,1536]{1,0:T(8,128)S(1)}, f32[128,1536]{1,0:T(8,128)}, u32[]{:S(2)}) copy-start(f32[128,1536]{1,0:T(8,128)} %reduce-scatter.8.cloned.1.call-done) | copy-start | bytes 2359300
  1096.1 3.1 copy-start.13
  1096.1 3.1 copy-start.14
  1096.2 4.0 copy-start.12
  1096.2 27.4 %copy-start.15 = (f32[128,512]{1,0:T(8,128)S(1)}, f32[128,512]{1,0:T(8,128)}, u32[]{:S(2)}) copy-start(f32[128,512]{1,0:T(8,128)} %get-tuple-element.7) | copy-start | bytes 786436
Sparse Core Ops, SparseCore 0:
  10.5 48.1 all-gather.18
  60.5 45.3 all-gather.20
  108.2 60.3 reduce-scatter.3
  170.4 45.2 all-gather.22
  217.9 60.3 reduce-scatter.5
  279.7 218.0 all-gather.28
  499.4 216.3 all-gather.24
  717.4 216.3 all-gather.26
  936.1 58.5 reduce-scatter.7
  1004.2 58.6 all-reduce.2
  1065.6 27.0 all-gather.14
  1096.2 27.3 all-gather.16
